TPU v7x, 16 devices: a whole 2x2x2 slice. The times are simulated.
16 devices in a mesh: tp: 16 (over z, y, x, core).
Axes of the slice: x: 2, y: 2, z: 2, core: 2. Of those that a mesh axis runs over, the one named last changes fastest.
Arguments:
- hidden: bfloat16 [4, 8192, 1024], P(None, 'tp')
- labels: int32 [4, 8192], P(None, 'tp')
- loss_mask: int32 [4, 8192], P(None, 'tp')
- norm_gain: float32 [1024], replicated
- w_head: bfloat16 [1024, 32768], P(None, 'tp')
Outputs:
- output 1: float32 [], replicated
- output 2: bfloat16 [4, 8192, 1024], P(None, 'tp')
- output 3: bfloat16 [1024, 32768], P(None, 'tp')
- output 4: float32 [1024], replicated
All inputs are finite; a program needn't handle non-finite values.
Results may differ from a plain program's by a relative error of at most 0.0086346.
Values are sent between devices in bfloat16 or wider.
A program may use at most 1 GiB of HBM per device.

v0:
```python
import jax
import jax.numpy as jnp
from jax import lax
from jax.sharding import PartitionSpec as P, NamedSharding

NORM_EPS = 1e-6


def rms_norm(x_rows, norm_gain):
    inv_rms = lax.rsqrt(jnp.mean(x_rows * x_rows, axis=-1, keepdims=True) + NORM_EPS)
    return x_rows * inv_rms * norm_gain


def solution(mesh):
    n_shards = mesh.shape['tp']

    def device_step(hidden, labels, loss_mask, norm_gain, w_head):
        batch_size, seq_loc, model_width = hidden.shape
        v_loc = w_head.shape[1]
        norm_loc, norm_vjp = jax.vjp(rms_norm, hidden.astype(jnp.float32), norm_gain)
        hn_all = lax.all_gather(norm_loc.astype(jnp.bfloat16), 'tp', axis=1, tiled=True)
        label_all = lax.all_gather(labels, 'tp', axis=1, tiled=True)
        mask_all = lax.all_gather(loss_mask, 'tp', axis=1, tiled=True)
        logits = jnp.einsum('btd,dv->btv', hn_all, w_head, preferred_element_type=jnp.float32)
        row_max = lax.pmax(jnp.max(logits, axis=-1), 'tp')
        sum_exp = lax.psum(jnp.sum(jnp.exp(logits - row_max[..., None]), axis=-1), 'tp')
        col_start = lax.axis_index('tp') * v_loc
        is_label = (lax.broadcasted_iota(jnp.int32, (1, 1, v_loc), 2) + col_start) == label_all[..., None]
        label_logit = lax.psum(jnp.sum(jnp.where(is_label, logits, 0.0), axis=-1), 'tp')
        log_norm = row_max + jnp.log(sum_exp)
        tok_weight = mask_all.astype(jnp.float32)
        kept_count = jnp.sum(tok_weight)
        mean_loss = jnp.sum(tok_weight * (log_norm - label_logit)) / kept_count
        tok_scale = tok_weight / kept_count
        d_logits = ((jnp.exp(logits - log_norm[..., None]) - is_label.astype(jnp.float32)) * tok_scale[..., None]).astype(jnp.bfloat16)
        d_head = jnp.einsum('btd,btv->dv', hn_all, d_logits, preferred_element_type=jnp.float32).astype(jnp.bfloat16)
        dhn_part = jnp.einsum('btv,dv->btd', d_logits, w_head, preferred_element_type=jnp.float32).astype(jnp.bfloat16)
        received = lax.all_to_all(dhn_part.reshape(batch_size, n_shards, seq_loc, model_width), 'tp', 1, 1, tiled=True)
        d_norm = jnp.sum(received, axis=1, dtype=jnp.float32)
        d_x, d_gain = norm_vjp(d_norm)
        d_gain = lax.psum(d_gain, 'tp')
        return mean_loss, d_x.astype(jnp.bfloat16), d_head, d_gain

    return jax.shard_map(device_step, mesh=mesh, in_specs=(P(None, 'tp', None), P(None, 'tp'), P(None, 'tp'), P(), P(None, 'tp')), out_specs=(P(), P(None, 'tp', None), P(None, 'tp'), P()), check_vma=False)
```

profile of v0, /device:TPU:0, one launch (start us, length us, event | category | flops | bytes accessed | tf_op | source)
XLA Modules:
  0.0 1829.5 jit_solution(13434139503216217277)
XLA Ops:
  7.2 3.1 fusion.9
  10.3 0.6 copy-done.3
  10.9 0.6 copy-done.1
  11.5 4.1 fusion.6
  15.7 0.0 all-reduce.4.cloned.1.call-start
  15.7 245.1 %all-gather.2.cloned.1.call-done = bf16[4,8192,1024]{2,1,0:T(8,128)(2,1)} async-done(((bf16[4,512,1024]{2,1,0:T(8,128)(2,1)}), bf16[4,8192,1024]{2,1,0:T(8,128)(2,1)}) %all-gather.2.cloned.1.call-update) | async-done | bytes 67108880 | tf_op jit(solution)/shard_map/all_gather | solution.py:21
  260.8 155.8 %fusion.15 = (f32[4,8192]{1,0:T(4,128)}, f32[4,8192,2048]{1,2,0:T(8,128)}) fusion(bf16[4,8192,1024]{2,1,0:T(8,128)(2,1)} %all-gather.2.cloned.1.call-done, bf16[1024,2048]{1,0:T(8,128)(2,1)} %param.9), kind=kOutput, calls=%fused_computation.33 | convolution fusion | flops 137506029568 | bytes 339869696 | tf_op jit(solution)/shard_map/btd,dv->btv/dot_general | solution.py:24
  416.7 13.1 all_gather.11
  429.8 49.8 %all-reduce.4.cloned.1.call-done = f32[4,8192]{1,0:T(4,128)} async-done(((f32[4,8192]{1,0:T(4,128)}), f32[4,8192]{1,0:T(4,128)}) %all-reduce.4.cloned.1.call-update) | async-done | bytes 131088 | tf_op jit(solution)/shard_map/pmax | solution.py:25
  479.6 85.6 %fusion = (f32[4,8192]{1,0:T(4,128)}, f32[4,8192]{1,0:T(4,128)}) fusion(f32[4,8192,2048]{1,2,0:T(8,128)} %get-tuple-element.14, s32[4,8192]{1,0:T(4,128)S(1)} %all_gather.11, s32[2048]{0:T(1024)S(1)} %iota_add_fusion, f32[4,8192]{1,0:T(4,128)} %all-reduce.4.cloned.1.call-done), kind=kLoop, calls=%fused_computation.2 | loop fusion | flops 335478784 | bytes 268967936 | tf_op jit(solution)/shard_map/reduce_sum | solution.py:29
  565.3 13.9 all_gather.9
  579.1 51.8 %all-reduce.6.cloned.1.call-done = (f32[4,8192]{1,0:T(4,128)}, f32[4,8192]{1,0:T(4,128)}) async-done(((f32[4,8192]{1,0:T(4,128)}, f32[4,8192]{1,0:T(4,128)}), (f32[4,8192]{1,0:T(4,128)}, f32[4,8192]{1,0:T(4,128)})) %all-reduce.6.cloned.1.call-update) | async-done | bytes 262160 | tf_op jit(solution)/shard_map/psum | solution.py:26
  630.9 1.7 convert_reduce_fusion.1
  632.6 0.7 convert_divide_fusion
  633.3 127.3 %fusion.3 = bf16[4,8192,2048]{1,2,0:T(8,128)(2,1)} fusion(f32[4,8192,2048]{1,2,0:T(8,128)} %get-tuple-element.14, f32[4,8192]{1,0:T(4,128)S(1)} %convert_divide_fusion, f32[4,8192]{1,0:T(4,128)S(1)} %get-tuple-element.12, s32[4,8192]{1,0:T(4,128)S(1)} %all_gather.11, s32[2048]{0:T(1024)S(1)} %iota_add_fusion), kind=kLoop, calls=%fused_computation.5 | loop fusion | flops 402653184 | bytes 403054592 | tf_op jit(solution)/shard_map/convert_element_type | solution.py:35
  760.5 150.2 %convolution_convert_fusion = bf16[4,8192,1024]{2,1,0:T(8,128)(2,1)} fusion(bf16[4,8192,2048]{1,2,0:T(8,128)(2,1)} %fusion.3, bf16[1024,2048]{1,0:T(8,128)(2,1)} %param.9), kind=kOutput, calls=%fused_computation.8 | convolution fusion | flops 137472507904 | bytes 205520896 | tf_op jit(solution)/shard_map/btv,dv->btd/dot_general | solution.py:37
  910.8 43.3 %copy.15 = bf16[4,16,512,1024]{3,2,0,1:T(8,128)(2,1)} copy(bf16[4,16,512,1024]{3,2,1,0:T(8,128)(2,1)} %bitcast.2) | data formatting | bytes 134217728 | tf_op jit(solution)/shard_map/reshape | solution.py:38
  954.1 6.2 all-to-all-start
  961.6 150.4 %bitcast_convert_fusion = bf16[1024,2048]{1,0:T(8,128)(2,1)} fusion(bf16[4,8192,1024]{2,1,0:T(8,128)(2,1)} %all-gather.2.cloned.1.call-done, bf16[4,8192,2048]{1,2,0:T(8,128)(2,1)} %fusion.3), kind=kOutput, calls=%fused_computation.21 | convolution fusion | flops 137441050624 | bytes 205520896 | tf_op jit(solution)/shard_map/btd,btv->dv/dot_general | solution.py:36
  1111.9 637.7 %all-to-all-done = bf16[4,16,512,1024]{3,2,0,1:T(8,128)(2,1)} async-done(((bf16[4,16,512,1024]{3,2,0,1:T(8,128)(2,1)}), bf16[4,16,512,1024]{3,2,0,1:T(8,128)(2,1)}, u32[]{:S(2)}, u32[]{:S(2)}) %all-to-all-start) | async-done | bytes 67108896 | tf_op jit(solution)/shard_map/all_to_all | solution.py:38
  1749.7 24.6 %convert_reduce_fusion = f32[4,512,1024]{2,1,0:T(8,128)} fusion(bf16[4,16,512,1024]{3,2,0,1:T(8,128)(2,1)} %all-to-all-done), kind=kLoop, calls=%fused_computation.7 | loop fusion | flops 65011712 | bytes 75497472 | tf_op jit(solution)/shard_map/reduce_sum | solution.py:39
  1774.3 6.5 fusion.7
  1780.8 33.8 %psum.23 = f32[1024]{0:T(1024)} all-reduce(f32[1024]{0:T(1024)S(1)} %get-tuple-element.6), channel_id=1, replica_groups=mesh['tp'=16] {'tp'}, use_global_device_ids=true, to_apply=%region_12.13 | all-reduce | flops 1024 | bytes 8192 | tf_op jit(solution)/shard_map/psum | solution.py:41
  1814.6 6.9 fusion.8
  (22 shorter events, 0.2 us)
Async XLA Ops:
  7.2 253.7 %all-gather.2.cloned.1.call-start = ((), (), s32[]{:S(2)}) async-start(), calls=%async_computation.1 | async-start | bytes 71303168 | tf_op jit(solution)/shard_map/all_gather | solution.py:21
  10.3 0.6 copy-start.3
  10.9 0.6 copy-start.1
  15.7 464.0 %all-reduce.4.cloned.1.call-start = ((), (), s32[]{:S(2)}) async-start(), calls=%async_computation.2 | async-start | bytes 262144 | tf_op jit(solution)/shard_map/pmax | solution.py:25
  260.8 155.9 %copy-start.6 = (s32[4,512]{1,0:T(4,128)S(1)}, s32[4,512]{1,0:T(4,128)}, u32[]{:S(2)}) copy-start(s32[4,512]{1,0:T(4,128)} %param.6) | copy-start | bytes 24580
  416.7 214.3 %all-reduce.6.cloned.1.call-start = ((), (), s32[]{:S(2)}) async-start(), calls=%async_computation.3 | async-start | bytes 524288 | tf_op jit(solution)/shard_map/psum | solution.py:26
  479.6 85.6 %copy-start.7 = (s32[4,512]{1,0:T(4,128)S(1)}, s32[4,512]{1,0:T(4,128)}, u32[]{:S(2)}) copy-start(s32[4,512]{1,0:T(4,128)} %param.7) | copy-start | bytes 24580
  479.6 151.3 %copy-start = (f32[4,8192]{1,0:T(4,128)S(1)}, f32[4,8192]{1,0:T(4,128)}, u32[]{:S(2)}) copy-start(f32[4,8192]{1,0:T(4,128)} %all-reduce.4.cloned.1.call-done) | copy-start | bytes 393220
  954.1 795.6 %all-to-all-start = ((bf16[4,16,512,1024]{3,2,0,1:T(8,128)(2,1)}), bf16[4,16,512,1024]{3,2,0,1:T(8,128)(2,1)}, u32[]{:S(2)}, u32[]{:S(2)}) async-start(bf16[4,16,512,1024]{3,2,0,1:T(8,128)(2,1)} %copy.15), calls=%async_computation | async-start | bytes 134217728 | tf_op jit(solution)/shard_map/all_to_all | solution.py:38
  1111.9 662.3 %copy-start.2 = (f32[4,512]{1,0:T(4,128)S(1)}, f32[4,512]{1,0:T(4,128)}, u32[]{:S(2)}) copy-start(f32[4,512]{1,0:T(4,128)} %copy-done.1) | copy-start | bytes 24580
  1111.9 662.3 %copy-start.5 = (f32[1024]{0:T(1024)S(1)}, f32[1024]{0:T(1024)}, u32[]{:S(2)}) copy-start(f32[1024]{0:T(1024)} %param.8) | copy-start | bytes 12292
  1774.3 40.4 %copy-start.4 = (f32[4,512]{1,0:T(4,128)S(1)}, f32[4,512]{1,0:T(4,128)}, u32[]{:S(2)}) copy-start(f32[4,512]{1,0:T(4,128)} %copy-done.3) | copy-start | bytes 24580
Sparse Core Ops, SparseCore 0:
  15.8 244.9 all-gather.1
  416.8 62.8 all-reduce.3
  565.4 65.4 all-reduce.5
where the time goes:
time: 1840 us; the launch traced here: 1830 us
  waiting for transfers between devices  984 us (53%)
  matrix products  456 us (25%)
  other arithmetic  260 us (14%)
  blocking collectives  60.8 us (3%)
  local copies, waits for them, and re-layouts  44.5 us (2%)
    all_to_all x1, waiting for transfers between devices, device_step(): lax.all_to_all(dhn_part.reshape(batch_size, n_shards, seq_loc, model_widt...  638 us
    all_gather x1, waiting for transfers between devices, device_step(): lax.all_gather(norm_loc.astype(jnp.bfloat16), 'tp', axis=1, tiled=True)  245 us
    dot_general x1, matrix products, device_step(): jnp.einsum('btd,dv->btv', hn_all, w_head, preferred_element_type=jnp.floa...  156 us
    dot_general x1, matrix products, device_step(): jnp.einsum('btd,btv->dv', hn_all, d_logits, preferred_element_type=jnp.fl...  150 us
    dot_general x1, matrix products, device_step(): jnp.einsum('btv,dv->btd', d_logits, w_head, preferred_element_type=jnp.fl...  150 us
    convert_element_type x1, other arithmetic, device_step(): ((jnp.exp(logits - log_norm[..., None]) - is_label.astype(jnp.float32)) *...  127 us
    reduce_sum x1, other arithmetic, device_step(): jnp.sum(jnp.where(is_label, logits, 0.0), axis=-1)  85.6 us
    psum x1, waiting for transfers between devices, device_step(): lax.psum(jnp.sum(jnp.exp(logits - row_max[..., None]), axis=-1), 'tp')  51.8 us
  transfers between devices with their start and end apart: 4, of which 4 were waited for; matrix products, arithmetic and copies ran while one was open for 8% of the time, Pallas kernels for 0%

commit v1 on v0

v1 whole, which is shorter than its diff:
```python
import functools

import jax
import jax.numpy as jnp
from jax import lax
from jax.experimental import pallas as pl
from jax.experimental.pallas import tpu as pltpu
from jax.sharding import PartitionSpec as P


NORM_EPS = 1e-6

CORE, X, Y, Z = 1, 2, 4, 8
TM1 = 256
TM2 = 512
NC = 512
LANES = 128
ROWS = 8


def rms_norm(x_rows, norm_gain):
    inv_rms = lax.rsqrt(jnp.mean(x_rows * x_rows, axis=-1, keepdims=True) + NORM_EPS)
    return x_rows * inv_rms * norm_gain


def columns_of(rows_ref):
    rows = rows_ref[...]
    return jnp.concatenate([rows, jnp.zeros((LANES - ROWS, rows.shape[1]), rows.dtype)]).T


def logits_kernel(parts, lane0, copy_hn, n_prev, *refs):
    rows_ref = refs[0]
    a_refs = refs[1:1 + len(parts)]
    w_refs = refs[1 + len(parts):3 + len(parts)]
    outs = refs[3 + len(parts) + n_prev:]
    z_ref, st_ref = outs[0], outs[1]
    if copy_hn:
        hn_ref = outs[2]
        i = pl.program_id(0)
        for a_ref, (lo, hi) in zip(a_refs, parts):
            @pl.when((i >= lo) & (i < hi))
            def _(a_ref=a_ref):
                hn_ref[...] = a_ref[...]
        a = hn_ref[...]
    else:
        a = a_refs[0][...]
    tm = a.shape[0]
    rows = columns_of(rows_ref)
    lane = lax.broadcasted_iota(jnp.int32, (tm, LANES), 1)
    lane_f = lane.astype(jnp.float32)
    m = jnp.full((tm, LANES), -jnp.inf, jnp.float32)
    s = jnp.zeros((tm, LANES), jnp.float32)
    lab = jnp.zeros((tm, LANES), jnp.float32)
    vloc = w_refs[0].shape[1]
    for k, w_ref in enumerate(w_refs):
        dist = jnp.broadcast_to(rows[:, lane0 + k:lane0 + k + 1], (tm, LANES)) - lane_f
        for j in range(vloc // NC):
            z = jnp.dot(a, w_ref[:, j * NC:(j + 1) * NC], preferred_element_type=jnp.float32)
            z_ref[:, k * vloc + j * NC:k * vloc + (j + 1) * NC] = z
            cols = [z[:, l * LANES:(l + 1) * LANES] for l in range(NC // LANES)]
            m_new = functools.reduce(jnp.maximum, cols, m)
            s = s * jnp.exp(m - m_new)
            for l, zc in enumerate(cols):
                s = s + jnp.exp(zc - m_new)
                lab = lab + jnp.where(dist == float(j * NC + l * LANES), zc, 0.0)
            m = m_new
    row_m = jnp.max(m, axis=1, keepdims=True)
    row_s = jnp.sum(s * jnp.exp(m - row_m), axis=1, keepdims=True)
    row_l = jnp.sum(lab, axis=1, keepdims=True)
    st_ref[...] = jnp.where(lane == 0, row_m, jnp.where(lane == 1, row_s, row_l)).T[:ROWS]


def logits_call(rows, a_list, w_pair, pair, row_off, n_rows, z_all, hn_all, copy_hn):
    tokens = rows.shape[1]
    d, vloc = w_pair[0].shape
    tiles, off = n_rows // TM1, row_off // TM1
    parts, lo = [], 0
    a_specs = []
    if copy_hn:
        for a in a_list:
            n = a.shape[0] // TM1
            parts.append((lo, lo + n))
            a_specs.append(pl.BlockSpec((TM1, d), lambda i, lo=lo, n=n: (jnp.clip(i - lo, 0, n - 1), 0)))
            lo += n
    else:
        parts.append((0, tiles))
        a_specs.append(pl.BlockSpec((TM1, d), lambda i: (i + off, 0)))
    in_specs = [pl.BlockSpec((ROWS, TM1), lambda i: (0, i + off))] + a_specs
    in_specs += [pl.BlockSpec((d, vloc), lambda i: (0, 0), pipeline_mode=pl.Buffered(1))] * 2
    args = [rows, *a_list, *w_pair]
    out_specs = [pl.BlockSpec((TM1, 2 * vloc), lambda i: (i + off, pair)), pl.BlockSpec((ROWS, TM1), lambda i: (0, i))]
    out_shape = [jax.ShapeDtypeStruct((tokens, 4 * vloc), jnp.float32), jax.ShapeDtypeStruct((ROWS, n_rows), jnp.float32)]
    aliases = {}
    if copy_hn:
        out_specs.append(pl.BlockSpec((TM1, d), lambda i: (i + off, 0)))
        out_shape.append(jax.ShapeDtypeStruct((tokens, d), jnp.bfloat16))
    n_prev = 0
    if z_all is not None:
        aliases[len(args)] = 0
        args.append(z_all)
        n_prev += 1
        if copy_hn:
            aliases[len(args)] = 2
            args.append(hn_all)
            n_prev += 1
    in_specs += [pl.BlockSpec(memory_space=pl.ANY)] * n_prev
    return pl.pallas_call(
        functools.partial(logits_kernel, tuple(parts), 2 * pair, copy_hn, n_prev),
        grid=(tiles,),
        in_specs=in_specs,
        out_specs=out_specs,
        out_shape=out_shape,
        input_output_aliases=aliases,
        compiler_params=pltpu.CompilerParams(dimension_semantics=("arbitrary",), vmem_limit_bytes=56 * 2**20),
        cost_estimate=pl.CostEstimate(
            flops=2 * n_rows * d * 2 * vloc, bytes_accessed=n_rows * 2 * vloc * 4, transcendentals=n_rows * 2 * vloc
        ),
    )(*args)


def grad_kernel(n_prev, rows_ref, z_ref, w0, w1, w2, w3, *refs):
    dz_ref, dhn_ref, w_scr, sem = refs[n_prev:]
    i, blk = pl.program_id(0), pl.program_id(1)

    @pl.when((i == 0) & (blk == 0))
    def _():
        for k, w in enumerate((w0, w1, w2, w3)):
            pltpu.make_async_copy(w, w_scr.at[k], sem.at[k]).start()

    @pl.when(i == 0)
    def _():
        pltpu.make_async_copy(w0, w_scr.at[blk], sem.at[blk]).wait()

    rows = columns_of(rows_ref)
    tm = rows.shape[0]
    lane = lax.broadcasted_iota(jnp.int32, (tm, LANES), 1)
    lab = jnp.sum(jnp.where(lane == blk, rows, 0.0), axis=1, keepdims=True)
    dist = jnp.broadcast_to(lab, (tm, LANES)) - lane.astype(jnp.float32)
    lse = jnp.broadcast_to(rows[:, 4:5], (tm, LANES))
    scale = jnp.broadcast_to(rows[:, 5:6], (tm, LANES))
    vloc = z_ref.shape[1]
    part = None
    for j in range(vloc // NC):
        cols = []
        for l in range(NC // LANES):
            lo = j * NC + l * LANES
            p = jnp.exp(z_ref[:, lo:lo + LANES] - lse)
            p = p - jnp.where(dist == float(lo), 1.0, 0.0)
            cols.append((p * scale).astype(jnp.bfloat16))
        dz = jnp.concatenate(cols, axis=1)
        dz_ref[:, j * NC:(j + 1) * NC] = dz
        prod = lax.dot_general(
            dz, w_scr[blk, :, j * NC:(j + 1) * NC], (((1,), (1,)), ((), ())), preferred_element_type=jnp.float32
        )
        part = prod if part is None else part + prod
    part = part.astype(jnp.bfloat16).astype(jnp.float32)

    @pl.when(blk == 0)
    def _():
        dhn_ref[...] = part

    @pl.when(blk != 0)
    def _():
        dhn_ref[...] += part


def grad_call(rows, z_all, w_list, row_off, n_rows, dz_all):
    tokens = rows.shape[1]
    d, vloc = w_list[0].shape
    tiles, off = n_rows // TM2, row_off // TM2
    any_spec = pl.BlockSpec(memory_space=pl.ANY)
    in_specs = [pl.BlockSpec((ROWS, TM2), lambda i, s: (0, i + off)), pl.BlockSpec((TM2, vloc), lambda i, s: (i + off, s))]
    in_specs += [any_spec] * 4
    args = [rows, z_all, *w_list]
    aliases, n_prev = {}, 0
    if dz_all is not None:
        aliases[len(args)] = 0
        args.append(dz_all)
        in_specs.append(any_spec)
        n_prev = 1
    return pl.pallas_call(
        functools.partial(grad_kernel, n_prev),
        grid=(tiles, 4),
        in_specs=in_specs,
        out_specs=[pl.BlockSpec((TM2, vloc), lambda i, s: (i + off, s)), pl.BlockSpec((TM2, d), lambda i, s: (i, 0))],
        out_shape=[jax.ShapeDtypeStruct((tokens, 4 * vloc), jnp.bfloat16), jax.ShapeDtypeStruct((n_rows, d), jnp.float32)],
        scratch_shapes=[pltpu.VMEM((4, d, vloc), jnp.bfloat16), pltpu.SemaphoreType.DMA((4,))],
        input_output_aliases=aliases,
        compiler_params=pltpu.CompilerParams(dimension_semantics=("arbitrary", "arbitrary"), vmem_limit_bytes=58 * 2**20),
        cost_estimate=pl.CostEstimate(
            flops=2 * n_rows * d * 4 * vloc, bytes_accessed=n_rows * 4 * vloc * 6, transcendentals=n_rows * 4 * vloc
        ),
    )(*args)


def head_kernel(own_ref, core_ref, x_ref, *refs):
    refs[-1][...] = (own_ref[...] + core_ref[...] + x_ref[...]).astype(jnp.bfloat16)


def head_call(own, from_core, from_x, k, prev):
    d, width = from_x.shape
    tile = min(TM1, d)
    wide = pl.BlockSpec((tile, width), lambda i: (i, k))
    args, in_specs, aliases = [own, from_core, from_x], [wide, wide, pl.BlockSpec((tile, width), lambda i: (i, 0))], {}
    if prev is not None:
        args.append(prev)
        in_specs.append(pl.BlockSpec(memory_space=pl.ANY))
        aliases = {3: 0}
    return pl.pallas_call(
        head_kernel,
        grid=(d // tile,),
        in_specs=in_specs,
        out_specs=wide,
        out_shape=jax.ShapeDtypeStruct(own.shape, jnp.bfloat16),
        input_output_aliases=aliases,
        compiler_params=pltpu.CompilerParams(dimension_semantics=("arbitrary",)),
        cost_estimate=pl.CostEstimate(flops=10**6, bytes_accessed=7 * 2**20, transcendentals=0),
    )(*args)


def rows_kernel(base_ref, pair_ref, far_ref, out_ref):
    half = pair_ref.shape[1] // 2
    for pos, (piece, h) in enumerate(ROW_ORDER):
        src = pair_ref if piece < 2 else far_ref
        k = 2 * (piece % 2)
        label = src[k:k + 1, h * half:(h + 1) * half]
        at = slice(pos * half, (pos + 1) * half)
        for q in range(4):
            out_ref[q:q + 1, at] = (label - base_ref[q]).astype(jnp.float32)
        out_ref[4:5, at] = src[k + 1:k + 2, h * half:(h + 1) * half].astype(jnp.float32)
        out_ref[5:, at] = jnp.zeros((ROWS - 5, half), jnp.float32)


def merge_rows(a, b):
    top = jnp.maximum(a[0:1], b[0:1])
    return top, a[1:2] * jnp.exp(a[0:1] - top) + b[1:2] * jnp.exp(b[0:1] - top), a[2:3] + b[2:3]


def local_stats_kernel(a, b, c, d, e, f, out_ref):
    half = a.shape[1] // 2
    first = [(a, 0), (a, 1), (b, 0), (b, 1), (c, 0), (c, 1), (e, 0), (e, 1)]
    second = [(d, k) for k in range(6)] + [(f, 0), (f, 1)]
    for pos, ((x, i), (y, j)) in enumerate(zip(first, second)):
        got = merge_rows(x[:, i * half:(i + 1) * half], y[:, j * half:(j + 1) * half])
        at = slice(pos * half, (pos + 1) * half)
        for k, v in enumerate(got):
            out_ref[k:k + 1, at] = v
        out_ref[3:, at] = jnp.zeros((ROWS - 3, half), jnp.float32)


def peer_stats_kernel(order, mine_ref, theirs_ref, out_ref):
    half = mine_ref.shape[1] // 8
    for pos, src in enumerate(order):
        at = slice(pos * half, (pos + 1) * half)
        got = merge_rows(mine_ref[:, at], theirs_ref[:, src * half:(src + 1) * half])
        for k, v in enumerate(got):
            out_ref[k:k + 1, at] = v
        out_ref[3:, at] = jnp.zeros((ROWS - 3, half), jnp.float32)


def last_stats_kernel(order, kept_ref, rows_ref, mine_ref, theirs_ref, out_ref):
    half = mine_ref.shape[1] // 8
    out_ref[...] = rows_ref[...]
    for pos, src in enumerate(order):
        at = slice(pos * half, (pos + 1) * half)
        top, total, label = merge_rows(mine_ref[:, at], theirs_ref[:, src * half:(src + 1) * half])
        out_ref[4:5, at] = top + jnp.log(total)
        out_ref[5:6, at] = rows_ref[4:5, at] / kept_ref[0]
        out_ref[6:7, at] = label


def small_call(kernel, *args, smem=0):
    width = max(a.shape[-1] for a in args[smem:])
    if kernel is local_stats_kernel or kernel is rows_kernel:
        width = 4 * args[1].shape[1]
    spaces = [pltpu.SMEM] * smem + [pltpu.VMEM] * (len(args) - smem)
    return pl.pallas_call(
        kernel,
        in_specs=[pl.BlockSpec(memory_space=m) for m in spaces],
        out_specs=pl.BlockSpec(memory_space=pltpu.VMEM),
        out_shape=jax.ShapeDtypeStruct((ROWS, width), jnp.float32),
        cost_estimate=pl.CostEstimate(flops=10**6, bytes_accessed=10**6, transcendentals=0),
    )(*args)


ROW_ORDER = ((0, 0), (0, 1), (1, 0), (2, 0), (1, 1), (2, 1), (3, 0), (3, 1))
FROM_Y = tuple(ROW_ORDER.index((p ^ 1, h)) for p, h in ROW_ORDER)
FROM_Z = tuple(ROW_ORDER.index((p ^ 2, h)) for p, h in ROW_ORDER)

CHUNKS = 4


def solution(mesh):
    n_dev = mesh.shape['tp']

    def swap(value, bit):
        return lax.ppermute(value, 'tp', [(i, i ^ bit) for i in range(n_dev)])

    def device_step(hidden, labels, loss_mask, norm_gain, w_head):
        batch, seq, d = hidden.shape
        vloc = w_head.shape[1]
        n_tok = batch * seq
        half = n_tok // 2
        me = lax.axis_index('tp')

        own = jnp.stack([labels.reshape(n_tok), loss_mask.reshape(n_tok)])
        near = jnp.concatenate([own, swap(own, Y)])
        far = swap(near, Z)
        base = jnp.stack([(me ^ q) * vloc for q in range(4)])
        rows1 = small_call(rows_kernel, base, near, far, smem=1)
        kept = jnp.sum((near[1::2] + far[1::2]).astype(jnp.float32)).reshape(1)
        kept = kept + swap(kept, CORE)
        kept = kept + swap(kept, X)

        w_core = swap(w_head, CORE)
        w_x = swap(w_head, X)
        x_rows = hidden.reshape(n_tok, d).astype(jnp.float32)
        hn0, hn1 = (rms_norm(x_rows[i:i + half], norm_gain).astype(jnp.bfloat16) for i in (0, half))
        y0, z0 = swap(hn0, Y), swap(hn0, Z)
        y1, z1 = swap(hn1, Y), swap(hn1, Z)
        d0, d1 = swap(z0, Y), swap(y1, Z)
        w_xc = swap(w_x, CORE)
        w_list = (w_head, w_core, w_x, w_xc)

        def logits(a_list, pair, index, count, z_all, hn_all):
            return logits_call(
                rows1, a_list or [hn_all], w_list[2 * pair:2 * pair + 2], pair, index * half, count * half,
                z_all, hn_all, bool(a_list),
            )

        z_all, st_a, hn_all = logits([hn0, hn1], 0, 0, 2, None, None)
        z_all, st_b, hn_all = logits([y0, z0], 0, 2, 2, z_all, hn_all)
        z_all, st_c, hn_all = logits([y1, z1], 0, 4, 2, z_all, hn_all)
        z_all, st_d = logits(None, 1, 0, 6, z_all, hn_all)
        z_all, st_e, hn_all = logits([d0, d1], 0, 6, 2, z_all, hn_all)
        z_all, st_f = logits(None, 1, 6, 2, z_all, hn_all)

        stats = small_call(local_stats_kernel, st_a, st_b, st_c, st_d, st_e, st_f)
        stats = small_call(functools.partial(peer_stats_kernel, FROM_Y), stats, swap(stats, Y))
        rows2 = small_call(functools.partial(last_stats_kernel, FROM_Z), kept, rows1, stats, swap(stats, Z), smem=1)
        loss_sum = jnp.sum(rows1[4, :n_tok] * (rows2[4, :n_tok] - rows2[6, :n_tok]))

        def grad(index, count, dz_all):
            return grad_call(rows2, z_all, w_list, index * half, count * half, dz_all)

        dz_all, g_d0 = grad(6, 1, None)
        got_z0 = swap(g_d0, Y)
        dz_all, g_d1 = grad(7, 1, dz_all)
        got_y1 = swap(g_d1, Z)
        dz_all, g_y0 = grad(2, 1, dz_all)
        own_y0 = swap(g_y0, Y)
        dz_all, g_z1 = grad(5, 1, dz_all)
        own_z1 = swap(g_z1, Z)
        dz_all, g_z0 = grad(3, 1, dz_all)
        own_z0 = swap(g_z0 + got_z0, Z)
        dz_all, g_y1 = grad(4, 1, dz_all)
        own_y1 = swap(g_y1 + got_y1, Y)
        dz_all, g_own = grad(0, 2, dz_all)

        def head_part(q, lo, size):
            dz = dz_all[:, q * vloc + lo:q * vloc + lo + size]
            return lax.dot_general(hn_all, dz, (((0,), (0,)), ((), ())), preferred_element_type=jnp.float32)

        vc = vloc // CHUNKS
        got_x = []
        for k in range(CHUNKS):
            from_core = swap(head_part(3, k * vc, vc), CORE)
            got_x.append(swap(head_part(2, k * vc, vc) + from_core, X))
        got_c = swap(head_part(1, 0, vloc), CORE)
        d_own = lax.optimization_barrier(head_part(0, 0, vloc))
        d_head = None
        for k in range(CHUNKS):
            d_head = head_call(d_own, got_c, got_x[k], k, d_head)

        d_norm = jnp.concatenate([g_own[:half] + own_y0 + own_z0, g_own[half:] + own_y1 + own_z1])
        _, norm_vjp = jax.vjp(rms_norm, x_rows, norm_gain)
        d_x, d_gain = norm_vjp(d_norm)
        sums = jnp.concatenate([d_gain, jnp.broadcast_to(loss_sum, (LANES,))])
        for bit in (CORE, Y, Z, X):
            sums = sums + swap(sums, bit)
        mean_loss = sums[d] / kept[0]
        return mean_loss, d_x.astype(jnp.bfloat16).reshape(batch, seq, d), d_head, sums[:d]

    return jax.shard_map(device_step, mesh=mesh, in_specs=(P(None, 'tp', None), P(None, 'tp'), P(None, 'tp'), P(), P(None, 'tp')), out_specs=(P(), P(None, 'tp', None), P(None, 'tp'), P()), check_vma=False)
```

time: 1840 us -> 1150 us (0.62)
  waiting for transfers between devices: 984 us -> 331 us
  Pallas kernels: 0 us -> 514 us
  matrix products: 456 us -> 209 us
  other arithmetic: 260 us -> 33.8 us
  blocking collectives: 60.8 us -> 0 us
  local copies, waits for them, and re-layouts: 44.5 us -> 10.6 us
  starting transfers between devices: 6.29 us -> 32.9 us
    all_to_all x1 -> x0, waiting for transfers between devices: 638 us -> none  [device_step(): lax.all_to_all(dhn_part.reshape(batch_size, n_shards, seq_loc, model_widt...]
    pallas_call x0 -> x21, Pallas kernels: none -> 514 us  [the longest x7 252 us: grad_call(): pl.pallas_call(functools.partial(grad_kernel, n_prev), grid=(tiles, 4), i...]
    ppermute x0 -> x34, waiting for transfers between devices: none -> 331 us  [swap(): return lax.ppermute(value, 'tp', [(i, i ^ bit) for i in range(n_dev)])]
    dot_general x3 -> x10, matrix products: 456 us -> 209 us  [head_part(): lax.dot_general(hn_all, dz, (((0,), (0,)), ((), ())), preferred_element_t...]
    all_gather x1 -> x0, waiting for transfers between devices: 245 us -> none  [device_step(): lax.all_gather(norm_loc.astype(jnp.bfloat16), 'tp', axis=1, tiled=True)]
    convert_element_type x3 -> x2, other arithmetic: 138 us -> 8.02 us  [the longest x1 4.97 us: device_step(): d_x.astype(jnp.bfloat16).reshape(batch, seq, d)]
    reduce_sum x3 -> x2, other arithmetic: 112 us -> 2.16 us  [the longest x1 1.54 us: device_step(): loss_sum = jnp.sum(rows1[4, :n_tok] * (rows2[4, :n_tok] - rows2[6, :n_tok]))]
    psum x1 -> x0, waiting for transfers between devices: 51.8 us -> none  [device_step(): lax.psum(jnp.sum(jnp.exp(logits - row_max[..., None]), axis=-1), 'tp')]
  transfers between devices with their start and end apart: 4 -> 34, of which waited for: 4 -> 11; matrix products, arithmetic and copies ran while one was open for 8% -> 18% of each run, Pallas kernels for 0% -> 17%
where the time goes in v1:
time: 1150 us; the launch traced here: 1140 us
  Pallas kernels  514 us (45%)
  waiting for transfers between devices  331 us (29%)
  matrix products  209 us (18%)
  other arithmetic  33.8 us (3%)
  starting transfers between devices  32.9 us (3%)
    ppermute x34, waiting for transfers between devices, swap(): return lax.ppermute(value, 'tp', [(i, i ^ bit) for i in range(n_dev)])  331 us
    pallas_call x7, Pallas kernels, grad_call(): pl.pallas_call(functools.partial(grad_kernel, n_prev), grid=(tiles, 4), i...  252 us
    pallas_call x6, Pallas kernels, logits_call(): pl.pallas_call(functools.partial(logits_kernel, tuple(parts), 2 * pair, c...  237 us
    dot_general x10, matrix products, head_part(): lax.dot_general(hn_all, dz, (((0,), (0,)), ((), ())), preferred_element_t...  209 us
    ppermute x34, starting transfers between devices, swap(): return lax.ppermute(value, 'tp', [(i, i ^ bit) for i in range(n_dev)])  32.9 us
  transfers between devices with their start and end apart: 34, of which 11 were waited for; matrix products, arithmetic and copies ran while one was open for 18% of the time, Pallas kernels for 17%

profile of v1, /device:TPU:0, one launch (start us, length us, event | category | flops | bytes accessed | tf_op | source)
XLA Modules:
  0.0 1136.1 jit_solution(12187712970759980654)
XLA Ops:
  14.6 45.9 %collective-permute-done = s32[2,2048]{1,0:T(2,128)S(1)} collective-permute-done((s32[2,2048]{1,0:T(2,128)S(1)}, s32[2,2048]{1,0:T(2,128)S(1)}, u32[]{:S(2)}, u32[]{:S(2)}) %collective-permute-start) | collective-permute-done | bytes 16416 | tf_op jit(solution)/shard_map/ppermute | solution.py:297
  70.7 24.8 %collective-permute-done.9.refs_2_.w2 = bf16[1024,2048]{1,0:T(8,128)(2,1)} collective-permute-done((bf16[1024,2048]{1,0:T(8,128)(2,1)}, bf16[1024,2048]{1,0:T(8,128)(2,1)}, u32[]{:S(2)}, u32[]{:S(2)}) %collective-permute-start.9) | collective-permute-done | bytes 4194336 | tf_op jit(solution)/shard_map/ppermute | solution.py:297
  95.4 31.7 %shard_map.85 = (f32[8192,8192]{1,0:T(8,128)}, f32[8,2048]{1,0:T(8,128)}, bf16[8192,1024]{1,0:T(8,128)(2,1)}) custom-call(f32[8,8192]{1,0:T(8,128)} %shard_map.84.refs_0_.rows_ref, bf16[1024,1024]{1,0:T(8,128)(2,1)} %get-tuple-element.75.refs_1_, bf16[1024,1024]{1,0:T(8,128)(2,1)} %get-tuple-element.74.refs_2_, bf16[1024,2048]{1,0:T(8,128)(2,1)} %w0.13, ...), custom_call_target="tpu_custom_call" | custom-call | flops 17179869184 | bytes 33554432 | tf_op jit(solution)/shard_map/pallas_call | solution.py:107
  128.4 31.7 %shard_map.86 = (f32[8192,8192]{1,0:T(8,128)}, f32[8,2048]{1,0:T(8,128)}, bf16[8192,1024]{1,0:T(8,128)(2,1)}) custom-call(f32[8,8192]{1,0:T(8,128)} %shard_map.84.refs_0_.rows_ref, bf16[1024,1024]{1,0:T(8,128)(2,1)} %copy-done.4, bf16[1024,1024]{1,0:T(8,128)(2,1)} %collective-permute-done.6.refs_2_, ...), custom_call_target="tpu_custom_call", output_to_operand_aliasing={{0}: (5, {}), {2}: (6, {})} | custom-call | flops 17179869184 | bytes 33554432 | tf_op jit(solution)/shard_map/pallas_call | solution.py:107
  161.4 31.7 %shard_map.87 = (f32[8192,8192]{1,0:T(8,128)}, f32[8,2048]{1,0:T(8,128)}, bf16[8192,1024]{1,0:T(8,128)(2,1)}) custom-call(f32[8,8192]{1,0:T(8,128)} %shard_map.84.refs_0_.rows_ref, bf16[1024,1024]{1,0:T(8,128)(2,1)} %collective-permute-done.7.refs_1_, bf16[1024,1024]{1,0:T(8,128)(2,1)} %copy-done.5, ...), custom_call_target="tpu_custom_call", output_to_operand_aliasing={{0}: (5, {}), {2}: (6, {})} | custom-call | flops 17179869184 | bytes 33554432 | tf_op jit(solution)/shard_map/pallas_call | solution.py:107
  193.1 80.2 %shard_map.88 = (f32[8192,8192]{1,0:T(8,128)}, f32[8,6144]{1,0:T(8,128)}) custom-call(f32[8,8192]{1,0:T(8,128)} %shard_map.84.refs_0_.rows_ref, bf16[8192,1024]{1,0:T(8,128)(2,1)} %get-tuple-element.41.refs_1_.refs_6_, bf16[1024,2048]{1,0:T(8,128)(2,1)} %collective-permute-done.9.refs_2_.w2, ...), custom_call_target="tpu_custom_call", output_to_operand_aliasing={{0}: (4, {})} | custom-call | flops 51539607552 | bytes 100663296 | tf_op jit(solution)/shard_map/pallas_call | solution.py:107
  273.4 31.7 %shard_map.89 = (f32[8192,8192]{1,0:T(8,128)}, f32[8,2048]{1,0:T(8,128)}, bf16[8192,1024]{1,0:T(8,128)(2,1)}) custom-call(f32[8,8192]{1,0:T(8,128)} %shard_map.84.refs_0_.rows_ref, bf16[1024,1024]{1,0:T(8,128)(2,1)} %collective-permute-done.11.refs_1_, ...), custom_call_target="tpu_custom_call", output_to_operand_aliasing={{0}: (5, {}), {2}: (6, {})} | custom-call | flops 17179869184 | bytes 33554432 | tf_op jit(solution)/shard_map/pallas_call | solution.py:107
  305.1 30.4 %shard_map.90 = (f32[8192,8192]{1,0:T(8,128)}, f32[8,2048]{1,0:T(8,128)}) custom-call(f32[8,8192]{1,0:T(8,128)} %shard_map.84.refs_0_.rows_ref, bf16[8192,1024]{1,0:T(8,128)(2,1)} %get-tuple-element.46.refs_1_, bf16[1024,2048]{1,0:T(8,128)(2,1)} %collective-permute-done.9.refs_2_.w2, ...), custom_call_target="tpu_custom_call", output_to_operand_aliasing={{0}: (4, {})} | custom-call | flops 17179869184 | bytes 33554432 | tf_op jit(solution)/shard_map/pallas_call | solution.py:107
  362.4 32.1 %shard_map.94 = (bf16[8192,8192]{1,0:T(8,128)(2,1)}, f32[1024,1024]{1,0:T(8,128)}) custom-call(f32[8,8192]{1,0:T(8,128)} %shard_map.93.rows_ref, f32[8192,8192]{1,0:T(8,128)} %get-tuple-element.49.z_ref, bf16[1024,2048]{1,0:T(8,128)(2,1)} %w0.13, bf16[1024,2048]{1,0:T(8,128)(2,1)} %collective-permute-done.4.refs_4_.w1, ...), custom_call_target="tpu_custom_call" | custom-call | flops 17179869184 | bytes 50331648 | tf_op jit(solution)/shard_map/pallas_call | solution.py:181
  394.5 32.6 %shard_map.95 = (bf16[8192,8192]{1,0:T(8,128)(2,1)}, f32[1024,1024]{1,0:T(8,128)}) custom-call(f32[8,8192]{1,0:T(8,128)} %shard_map.93.rows_ref, f32[8192,8192]{1,0:T(8,128)} %get-tuple-element.49.z_ref, bf16[1024,2048]{1,0:T(8,128)(2,1)} %w0.13, bf16[1024,2048]{1,0:T(8,128)(2,1)} %collective-permute-done.4.refs_4_.w1, ...), custom_call_target="tpu_custom_call", output_to_operand_aliasing={{0}: (6, {})} | custom-call | flops 17179869184 | bytes 50331648 | tf_op jit(solution)/shard_map/pallas_call | solution.py:181
  427.1 32.2 %shard_map.96 = (bf16[8192,8192]{1,0:T(8,128)(2,1)}, f32[1024,1024]{1,0:T(8,128)}) custom-call(f32[8,8192]{1,0:T(8,128)} %shard_map.93.rows_ref, f32[8192,8192]{1,0:T(8,128)} %get-tuple-element.49.z_ref, bf16[1024,2048]{1,0:T(8,128)(2,1)} %w0.13, bf16[1024,2048]{1,0:T(8,128)(2,1)} %collective-permute-done.4.refs_4_.w1, ...), custom_call_target="tpu_custom_call", output_to_operand_aliasing={{0}: (6, {})} | custom-call | flops 17179869184 | bytes 50331648 | tf_op jit(solution)/shard_map/pallas_call | solution.py:181
  459.3 32.3 %shard_map.97 = (bf16[8192,8192]{1,0:T(8,128)(2,1)}, f32[1024,1024]{1,0:T(8,128)}) custom-call(f32[8,8192]{1,0:T(8,128)} %shard_map.93.rows_ref, f32[8192,8192]{1,0:T(8,128)} %get-tuple-element.49.z_ref, bf16[1024,2048]{1,0:T(8,128)(2,1)} %w0.13, bf16[1024,2048]{1,0:T(8,128)(2,1)} %collective-permute-done.4.refs_4_.w1, ...), custom_call_target="tpu_custom_call", output_to_operand_aliasing={{0}: (6, {})} | custom-call | flops 17179869184 | bytes 50331648 | tf_op jit(solution)/shard_map/pallas_call | solution.py:181
  491.6 32.2 %shard_map.98 = (bf16[8192,8192]{1,0:T(8,128)(2,1)}, f32[1024,1024]{1,0:T(8,128)}) custom-call(f32[8,8192]{1,0:T(8,128)} %shard_map.93.rows_ref, f32[8192,8192]{1,0:T(8,128)} %get-tuple-element.49.z_ref, bf16[1024,2048]{1,0:T(8,128)(2,1)} %w0.13, bf16[1024,2048]{1,0:T(8,128)(2,1)} %collective-permute-done.4.refs_4_.w1, ...), custom_call_target="tpu_custom_call", output_to_operand_aliasing={{0}: (6, {})} | custom-call | flops 17179869184 | bytes 50331648 | tf_op jit(solution)/shard_map/pallas_call | solution.py:181
  523.8 32.4 %shard_map.99 = (bf16[8192,8192]{1,0:T(8,128)(2,1)}, f32[1024,1024]{1,0:T(8,128)}) custom-call(f32[8,8192]{1,0:T(8,128)} %shard_map.93.rows_ref, f32[8192,8192]{1,0:T(8,128)} %get-tuple-element.49.z_ref, bf16[1024,2048]{1,0:T(8,128)(2,1)} %w0.13, bf16[1024,2048]{1,0:T(8,128)(2,1)} %collective-permute-done.4.refs_4_.w1, ...), custom_call_target="tpu_custom_call", output_to_operand_aliasing={{0}: (6, {})} | custom-call | flops 17179869184 | bytes 50331648 | tf_op jit(solution)/shard_map/pallas_call | solution.py:181
  556.2 58.1 %shard_map.100 = (bf16[8192,8192]{1,0:T(8,128)(2,1)}, f32[2048,1024]{1,0:T(8,128)}) custom-call(f32[8,8192]{1,0:T(8,128)} %shard_map.93.rows_ref, f32[8192,8192]{1,0:T(8,128)} %get-tuple-element.49.z_ref, bf16[1024,2048]{1,0:T(8,128)(2,1)} %w0.13, bf16[1024,2048]{1,0:T(8,128)(2,1)} %collective-permute-done.4.refs_4_.w1, ...), custom_call_target="tpu_custom_call", output_to_operand_aliasing={{0}: (6, {})} | custom-call | flops 34359738368 | bytes 100663296 | tf_op jit(solution)/shard_map/pallas_call | solution.py:181
  659.5 44.2 %fusion = f32[1024,2048]{1,0:T(8,128)} fusion(bf16[8192,1024]{1,0:T(8,128)(2,1)} %get-tuple-element.46.refs_1_, bf16[8192,8192]{1,0:T(8,128)(2,1)} %get-tuple-element.63), kind=kOutput, calls=%fused_computation | convolution fusion | flops 34359738368 | bytes 58720256 | tf_op jit(solution)/shard_map/dot_general | solution.py:362
  703.7 45.4 %collective-permute-done.16 = f32[1024,1024]{1,0:T(8,128)S(1)} collective-permute-done((f32[1024,1024]{1,0:T(8,128)}, f32[1024,1024]{1,0:T(8,128)S(1)}, u32[]{:S(2)}, u32[]{:S(2)}) %collective-permute-start.16) | collective-permute-done | bytes 4194336 | tf_op jit(solution)/shard_map/ppermute | solution.py:297
  751.2 89.9 %collective-permute-done.18 = f32[1024,1024]{1,0:T(8,128)} collective-permute-done((f32[1024,1024]{1,0:T(8,128)}, f32[1024,1024]{1,0:T(8,128)}, u32[]{:S(2)}, u32[]{:S(2)}) %collective-permute-start.18) | collective-permute-done | bytes 4194336 | tf_op jit(solution)/shard_map/ppermute | solution.py:297
  861.7 16.1 %fusion.27 = f32[1024,512]{1,0:T(8,128)} fusion(f32[1024,512]{1,0:T(8,128)} %collective-permute-done.26, bf16[8192,1024]{1,0:T(8,128)(2,1)} %get-tuple-element.46.refs_1_, bf16[8192,8192]{1,0:T(8,128)(2,1)} %get-tuple-element.63), kind=kOutput, calls=%fused_computation.38 | convolution fusion | flops 8590458880 | bytes 29360128 | tf_op jit(solution)/shard_map/dot_general | solution.py:362
  878.4 50.4 %collective-permute-done.17 = f32[1024,1024]{1,0:T(8,128)S(1)} collective-permute-done((f32[1024,1024]{1,0:T(8,128)S(1)}, f32[1024,1024]{1,0:T(8,128)S(1)}, u32[]{:S(2)}, u32[]{:S(2)}) %collective-permute-start.17) | collective-permute-done | bytes 4194336 | tf_op jit(solution)/shard_map/ppermute | solution.py:297
  957.0 16.3 %fusion.30 = f32[1024,512]{1,0:T(8,128)} fusion(f32[1024,512]{1,0:T(8,128)} %collective-permute-done.28, bf16[8192,1024]{1,0:T(8,128)(2,1)} %get-tuple-element.46.refs_1_, bf16[8192,8192]{1,0:T(8,128)(2,1)} %get-tuple-element.63), kind=kOutput, calls=%fused_computation.39 | convolution fusion | flops 8590458880 | bytes 29360128 | tf_op jit(solution)/shard_map/dot_general | solution.py:362
  993.2 16.2 %fusion.33 = f32[1024,512]{1,0:T(8,128)} fusion(f32[1024,512]{1,0:T(8,128)} %collective-permute-done.30, bf16[8192,1024]{1,0:T(8,128)(2,1)} %get-tuple-element.46.refs_1_, bf16[8192,8192]{1,0:T(8,128)(2,1)} %get-tuple-element.63), kind=kOutput, calls=%fused_computation.40 | convolution fusion | flops 8590458880 | bytes 29360128 | tf_op jit(solution)/shard_map/dot_general | solution.py:362
  1009.8 57.5 %collective-permute-done.33.x_ref = f32[1024,512]{1,0:T(8,128)} collective-permute-done((f32[1024,512]{1,0:T(8,128)S(1)}, f32[1024,512]{1,0:T(8,128)}, u32[]{:S(2)}, u32[]{:S(2)}) %collective-permute-start.33) | collective-permute-done | bytes 2097184 | tf_op jit(solution)/shard_map/ppermute | solution.py:297
  1069.7 44.1 %fusion.2.own_ref = f32[1024,2048]{1,0:T(8,128)} fusion(bf16[8192,1024]{1,0:T(8,128)(2,1)} %get-tuple-element.46.refs_1_, bf16[8192,8192]{1,0:T(8,128)(2,1)} %get-tuple-element.63), kind=kOutput, calls=%fused_computation.2 | convolution fusion | flops 34359738368 | bytes 58720256 | tf_op jit(solution)/shard_map/dot_general | solution.py:362
  (137 shorter events, 191.1 us)
Async XLA Ops:
  0.6 68.4 %collective-permute-start.4 = (bf16[1024,2048]{1,0:T(8,128)(2,1)}, bf16[1024,2048]{1,0:T(8,128)(2,1)}, u32[]{:S(2)}, u32[]{:S(2)}) collective-permute-start(bf16[1024,2048]{1,0:T(8,128)(2,1)} %w0.13), channel_id=1, source_target_pairs={{0,1},{1,0},{2,3},{3,2},{4,5},{5,4},{6,7},{7,6},{8,9},{9,8},{10,11... | collective-permute-start | bytes 12582920 | tf_op jit(solution)/shard_map/ppermute | solution.py:297
  1.4 94.0 %collective-permute-start.9 = (bf16[1024,2048]{1,0:T(8,128)(2,1)}, bf16[1024,2048]{1,0:T(8,128)(2,1)}, u32[]{:S(2)}, u32[]{:S(2)}) collective-permute-start(bf16[1024,2048]{1,0:T(8,128)(2,1)} %w0.13), channel_id=1, source_target_pairs={{0,2},{1,3},{2,0},{3,1},{4,6},{5,7},{6,4},{7,5},{8,10},{9,11},{10,... | collective-permute-start | bytes 12582920 | tf_op jit(solution)/shard_map/ppermute | solution.py:297
  10.9 57.2 %collective-permute-start.6 = (bf16[1024,1024]{1,0:T(8,128)(2,1)}, bf16[1024,1024]{1,0:T(8,128)(2,1)}, u32[]{:S(2)}, u32[]{:S(2)}) collective-permute-start(bf16[1024,1024]{1,0:T(8,128)(2,1)} %get-tuple-element.75.refs_1_), channel_id=1, source_target_pairs={{0,8},{1,9},{2,10},{3,11},{4,12},{5,13},{6,14},{7,15},{8,0},{9,1},... | collective-permute-start | bytes 6291464 | tf_op jit(solution)/shard_map/ppermute | solution.py:297
  12.5 56.1 %collective-permute-start.7 = (bf16[1024,1024]{1,0:T(8,128)(2,1)}, bf16[1024,1024]{1,0:T(8,128)(2,1)}, u32[]{:S(2)}, u32[]{:S(2)}) collective-permute-start(bf16[1024,1024]{1,0:T(8,128)(2,1)} %get-tuple-element.74.refs_2_), channel_id=1, source_target_pairs={{0,4},{1,5},{2,6},{3,7},{4,0},{5,1},{6,2},{7,3},{8,12},{9,13},{10,... | collective-permute-start | bytes 6291464 | tf_op jit(solution)/shard_map/ppermute | solution.py:297
  64.5 62.6 %collective-permute-start.5 = (bf16[1024,1024]{1,0:T(8,128)(2,1)}, bf16[1024,1024]{1,0:T(8,128)(2,1)S(1)}, u32[]{:S(2)}, u32[]{:S(2)}) collective-permute-start(bf16[1024,1024]{1,0:T(8,128)(2,1)} %get-tuple-element.75.refs_1_), channel_id=1, source_target_pairs={{0,4},{1,5},{2,6},{3,7},{4,0},{5,1},{6,2},{7,3},{8,12},{9,13},{10,... | collective-permute-start | bytes 6291464 | tf_op jit(solution)/shard_map/ppermute | solution.py:297
  68.1 92.0 %collective-permute-start.8 = (bf16[1024,1024]{1,0:T(8,128)(2,1)}, bf16[1024,1024]{1,0:T(8,128)(2,1)S(1)}, u32[]{:S(2)}, u32[]{:S(2)}) collective-permute-start(bf16[1024,1024]{1,0:T(8,128)(2,1)} %get-tuple-element.74.refs_2_), channel_id=1, source_target_pairs={{0,8},{1,9},{2,10},{3,11},{4,12},{5,13},{6,14},{7,15},{8,0},{9,1},... | collective-permute-start | bytes 6291464 | tf_op jit(solution)/shard_map/ppermute | solution.py:297
  68.6 204.8 %collective-permute-start.11 = (bf16[1024,1024]{1,0:T(8,128)(2,1)}, bf16[1024,1024]{1,0:T(8,128)(2,1)}, u32[]{:S(2)}, u32[]{:S(2)}) collective-permute-start(bf16[1024,1024]{1,0:T(8,128)(2,1)} %collective-permute-done.6.refs_2_), channel_id=1, source_target_pairs={{0,4},{1,5},{2,6},{3,7},{4,0},{5,1},{6,2},{7,3},{8,12},{9,13},{10,... | collective-permute-start | bytes 6291464 | tf_op jit(solution)/shard_map/ppermute | solution.py:297
  69.1 204.3 %collective-permute-start.12 = (bf16[1024,1024]{1,0:T(8,128)(2,1)}, bf16[1024,1024]{1,0:T(8,128)(2,1)}, u32[]{:S(2)}, u32[]{:S(2)}) collective-permute-start(bf16[1024,1024]{1,0:T(8,128)(2,1)} %collective-permute-done.7.refs_1_), channel_id=1, source_target_pairs={{0,8},{1,9},{2,10},{3,11},{4,12},{5,13},{6,14},{7,15},{8,0},{9,1},... | collective-permute-start | bytes 6291464 | tf_op jit(solution)/shard_map/ppermute | solution.py:297
  95.4 97.7 %collective-permute-start.10 = (bf16[1024,2048]{1,0:T(8,128)(2,1)}, bf16[1024,2048]{1,0:T(8,128)(2,1)}, u32[]{:S(2)}, u32[]{:S(2)}) collective-permute-start(bf16[1024,2048]{1,0:T(8,128)(2,1)} %collective-permute-done.9.refs_2_.w2), channel_id=1, source_target_pairs={{0,1},{1,0},{2,3},{3,2},{4,5},{5,4},{6,7},{7,6},{8,9},{9,8},{10,11... | collective-permute-start | bytes 12582920 | tf_op jit(solution)/shard_map/ppermute | solution.py:297
  655.4 93.7 %collective-permute-start.16 = (f32[1024,1024]{1,0:T(8,128)}, f32[1024,1024]{1,0:T(8,128)S(1)}, u32[]{:S(2)}, u32[]{:S(2)}) collective-permute-start(f32[1024,1024]{1,0:T(8,128)} %get-tuple-element.59), channel_id=1, source_target_pairs={{0,4},{1,5},{2,6},{3,7},{4,0},{5,1},{6,2},{7,3},{8,12},{9,13},{10,... | collective-permute-start | bytes 12582920 | tf_op jit(solution)/shard_map/ppermute | solution.py:297
  656.9 220.9 %collective-permute-start.15 = (f32[1024,1024]{1,0:T(8,128)}, f32[1024,1024]{1,0:T(8,128)}, u32[]{:S(2)}, u32[]{:S(2)}) collective-permute-start(f32[1024,1024]{1,0:T(8,128)} %get-tuple-element.57), channel_id=1, source_target_pairs={{0,4},{1,5},{2,6},{3,7},{4,0},{5,1},{6,2},{7,3},{8,12},{9,13},{10,... | collective-permute-start | bytes 12582920 | tf_op jit(solution)/shard_map/ppermute | solution.py:297
  657.5 220.9 %collective-permute-start.20 = (f32[1024,1024]{1,0:T(8,128)}, f32[1024,1024]{1,0:T(8,128)}, u32[]{:S(2)}, u32[]{:S(2)}) collective-permute-start(f32[1024,1024]{1,0:T(8,128)} %get-tuple-element.62), channel_id=1, source_target_pairs={{0,8},{1,9},{2,10},{3,11},{4,12},{5,13},{6,14},{7,15},{8,0},{9,1},... | collective-permute-start | bytes 12582920 | tf_op jit(solution)/shard_map/ppermute | solution.py:297
  658.1 183.0 %collective-permute-start.18 = (f32[1024,1024]{1,0:T(8,128)}, f32[1024,1024]{1,0:T(8,128)}, u32[]{:S(2)}, u32[]{:S(2)}) collective-permute-start(f32[1024,1024]{1,0:T(8,128)} %get-tuple-element.61), channel_id=1, source_target_pairs={{0,8},{1,9},{2,10},{3,11},{4,12},{5,13},{6,14},{7,15},{8,0},{9,1},... | collective-permute-start | bytes 12582920 | tf_op jit(solution)/shard_map/ppermute | solution.py:297
  659.5 202.2 %collective-permute-start.26 = (f32[1024,512]{1,0:T(8,128)}, f32[1024,512]{1,0:T(8,128)}, u32[]{:S(2)}, u32[]{:S(2)}) collective-permute-start(f32[1024,512]{1,0:T(8,128)} %fusion.17), channel_id=1, source_target_pairs={{0,1},{1,0},{2,3},{3,2},{4,5},{5,4},{6,7},{7,6},{8,9},{9,8},{10,11... | collective-permute-start | bytes 6291464 | tf_op jit(solution)/shard_map/ppermute | solution.py:297
  750.5 178.3 %collective-permute-start.17 = (f32[1024,1024]{1,0:T(8,128)S(1)}, f32[1024,1024]{1,0:T(8,128)S(1)}, u32[]{:S(2)}, u32[]{:S(2)}) collective-permute-start(f32[1024,1024]{1,0:T(8,128)S(1)} %add.91), channel_id=1, source_target_pairs={{0,8},{1,9},{2,10},{3,11},{4,12},{5,13},{6,14},{7,15},{8,0},{9,1},... | collective-permute-start | bytes 12582920 | tf_op jit(solution)/shard_map/ppermute | solution.py:297
  844.2 88.4 %collective-permute-start.19 = (f32[1024,1024]{1,0:T(8,128)S(1)}, f32[1024,1024]{1,0:T(8,128)}, u32[]{:S(2)}, u32[]{:S(2)}) collective-permute-start(f32[1024,1024]{1,0:T(8,128)S(1)} %add.93), channel_id=1, source_target_pairs={{0,4},{1,5},{2,6},{3,7},{4,0},{5,1},{6,2},{7,3},{8,12},{9,13},{10,... | collective-permute-start | bytes 12582920 | tf_op jit(solution)/shard_map/ppermute | solution.py:297
  861.7 252.0 %collective-permute-start.25 = (f32[1024,2048]{1,0:T(8,128)}, f32[1024,2048]{1,0:T(8,128)}, u32[]{:S(2)}, u32[]{:S(2)}) collective-permute-start(f32[1024,2048]{1,0:T(8,128)} %fusion), channel_id=1, source_target_pairs={{0,1},{1,0},{2,3},{3,2},{4,5},{5,4},{6,7},{7,6},{8,9},{9,8},{10,11... | collective-permute-start | bytes 25165832 | tf_op jit(solution)/shard_map/ppermute | solution.py:297
  877.8 79.2 %collective-permute-start.28 = (f32[1024,512]{1,0:T(8,128)}, f32[1024,512]{1,0:T(8,128)}, u32[]{:S(2)}, u32[]{:S(2)}) collective-permute-start(f32[1024,512]{1,0:T(8,128)} %fusion.13), channel_id=1, source_target_pairs={{0,1},{1,0},{2,3},{3,2},{4,5},{5,4},{6,7},{7,6},{8,9},{9,8},{10,11... | collective-permute-start | bytes 6291464 | tf_op jit(solution)/shard_map/ppermute | solution.py:297
  878.3 114.5 %collective-permute-start.30 = (f32[1024,512]{1,0:T(8,128)}, f32[1024,512]{1,0:T(8,128)}, u32[]{:S(2)}, u32[]{:S(2)}) collective-permute-start(f32[1024,512]{1,0:T(8,128)} %fusion.9), channel_id=1, source_target_pairs={{0,1},{1,0},{2,3},{3,2},{4,5},{5,4},{6,7},{7,6},{8,9},{9,8},{10,11... | collective-permute-start | bytes 6291464 | tf_op jit(solution)/shard_map/ppermute | solution.py:297
  932.7 195.6 %collective-permute-start.27 = (f32[1024,512]{1,0:T(8,128)}, f32[1024,512]{1,0:T(8,128)}, u32[]{:S(2)}, u32[]{:S(2)}) collective-permute-start(f32[1024,512]{1,0:T(8,128)} %fusion.27), channel_id=1, source_target_pairs={{0,2},{1,3},{2,0},{3,1},{4,6},{5,7},{6,4},{7,5},{8,10},{9,11},{10,... | collective-permute-start | bytes 6291464 | tf_op jit(solution)/shard_map/ppermute | solution.py:297
  973.4 149.1 %collective-permute-start.29 = (f32[1024,512]{1,0:T(8,128)}, f32[1024,512]{1,0:T(8,128)S(1)}, u32[]{:S(2)}, u32[]{:S(2)}) collective-permute-start(f32[1024,512]{1,0:T(8,128)} %fusion.30), channel_id=1, source_target_pairs={{0,2},{1,3},{2,0},{3,1},{4,6},{5,7},{6,4},{7,5},{8,10},{9,11},{10,... | collective-permute-start | bytes 6291464 | tf_op jit(solution)/shard_map/ppermute | solution.py:297
  991.3 76.0 %collective-permute-start.33 = (f32[1024,512]{1,0:T(8,128)S(1)}, f32[1024,512]{1,0:T(8,128)}, u32[]{:S(2)}, u32[]{:S(2)}) collective-permute-start(f32[1024,512]{1,0:T(8,128)S(1)} %fusion.36), channel_id=1, source_target_pairs={{0,2},{1,3},{2,0},{3,1},{4,6},{5,7},{6,4},{7,5},{8,10},{9,11},{10,... | collective-permute-start | bytes 6291464 | tf_op jit(solution)/shard_map/ppermute | solution.py:297
  1009.3 108.8 %collective-permute-start.31 = (f32[1024,512]{1,0:T(8,128)}, f32[1024,512]{1,0:T(8,128)}, u32[]{:S(2)}, u32[]{:S(2)}) collective-permute-start(f32[1024,512]{1,0:T(8,128)} %fusion.33), channel_id=1, source_target_pairs={{0,2},{1,3},{2,0},{3,1},{4,6},{5,7},{6,4},{7,5},{8,10},{9,11},{10,... | collective-permute-start | bytes 6291464 | tf_op jit(solution)/shard_map/ppermute | solution.py:297
  1067.3 65.4 %collective-permute-start.24 = (f32[1152]{0:T(1024)S(1)}, f32[1152]{0:T(1024)S(1)}, u32[]{:S(2)}, u32[]{:S(2)}) collective-permute-start(f32[1152]{0:T(1024)S(1)} %add.98), channel_id=1, source_target_pairs={{0,2},{1,3},{2,0},{3,1},{4,6},{5,7},{6,4},{7,5},{8,10},{9,11},{10,... | collective-permute-start | bytes 13832 | tf_op jit(solution)/shard_map/ppermute | solution.py:297
  (27 other events, 539.6 us)
